TPU v7x, 128 devices: a whole 4x4x4 slice. The times are simulated.
128 devices in a mesh: depth: 8 (over y, core), lat: 16 (over z, x).
Axes of the slice: x: 4, y: 4, z: 4, core: 2. Of those that a mesh axis runs over, the one named last changes fastest.
Arguments:
- emission: float32 [1024, 16, 2048], P('depth', None, 'lat'), may hold values from 0 to 2
- absorption: float32 [1024, 16, 2048], P('depth', None, 'lat'), may hold values from -4 to 4
- target: float32 [3, 16, 2048], P(None, None, 'lat'), may hold values from 0.2 to 0.8
- shift_whole: int32 [3, 1024], P(None, 'depth'), may hold values from -30 to 30, as said below
- shift_fraction: int32 [3, 1024], P(None, 'depth'), may hold values from 0 to 7, as said below
- taps_table: float32 [8, 4], replicated, may hold values from 0.05 to 0.45
Outputs:
- fitted_emission: float32 [1024, 16, 2048], P('depth', None, 'lat')
- fitted_absorption: float32 [1024, 16, 2048], P('depth', None, 'lat')
Inputs may be any that keep to these rules, and one draw needn't show every extreme that they name: `shift_whole`: both ends of the range are taken in every draw. `shift_fraction`: every value of the range is taken in every draw.
All inputs are finite; a program needn't handle non-finite values.
Results may differ from a plain program's by a relative error of at most 0.0003.
Values sent between devices are 32-bit elements; how exact they have to be, the bound alone decides.
No kernel may reach another device: no remote copies, remote signals or barrier semaphores. Data moves between devices by JAX's collectives and lax.ppermute only.
A program may use at most 128 MiB of HBM per device.

v0:
```python
import jax
import jax.numpy as jnp
from jax import lax
from jax.sharding import PartitionSpec as P

REACH = 32
ITERS = 3
HIGHEST = lax.Precision.HIGHEST
LEARN_RATE = 0.1
BETA_FIRST = 0.9
BETA_SECOND = 0.999
ADAM_EPSILON = 0.001


def copy_for_each(x, axis):
    devices = lax.axis_size(axis)
    return lax.all_to_all(jnp.broadcast_to(x[None], (devices, *x.shape)), axis, 0, 0, tiled=True)


def all_in_one(x, axis):
    leaves = jax.tree.leaves(x)
    sequence = sorted(range(len(leaves)), key=lambda k: -leaves[k].size)
    width = (1, *leaves[sequence[0]].shape)[-1]
    lines = [
        jnp.pad(leaves[k].reshape(-1), (0, -leaves[k].size % width)).reshape(-1, width)
        for k in sequence
    ]
    both, at, found = (copy_for_each(jnp.concatenate(lines), axis), 0, {})
    for k, line in zip(sequence, lines):
        slab = both[:, at : at + len(line)].reshape(len(both), -1)
        found[k] = slab[:, : leaves[k].size].reshape(-1, *leaves[k].shape)
        at += len(line)
    numbers = iter(range(len(leaves)))
    return jax.tree.map(lambda _: found[next(numbers)], x)


def once_a_type(x, axis):
    leaves, found = (jax.tree.leaves(x), {})
    for leading, a in enumerate(leaves):
        if leading not in found:
            alike = [k for k, b in enumerate(leaves) if b.dtype == a.dtype]
            got = (
                all_in_one([leaves[k] for k in alike], axis)
                if len(alike) > 1
                else [copy_for_each(a, axis)]
            )
            for k, b in zip(alike, got):
                found[k] = b
    numbers = iter(range(len(leaves)))
    return jax.tree.map(lambda _: found[next(numbers)], x)


def combined_pairwise(pieces, combine):
    while len(jax.tree.leaves(pieces)[0]) > 1:
        pieces = jax.vmap(combine)(
            *(jax.tree.map(lambda part: part[side::2], pieces) for side in (0, 1))
        )
    return jax.tree.map(lambda part: part[0], pieces)


def carried_in(x, axis, combine, identity, reverse):
    devices, here = (lax.axis_size(axis), lax.axis_index(axis))
    passed = jnp.arange(devices) > here if reverse else jnp.arange(devices) < here

    def kept(part, zero, own):
        part = jnp.where(
            passed.reshape(-1, *(1 for _ in own.shape)), part, jnp.asarray(zero, own.dtype)
        )
        return part[::-1] if reverse else part

    pieces = once_a_type(x, axis)
    return combined_pairwise(jax.tree.map(kept, pieces, identity, x), combine)


def plane_taps(fractions, taps_table):
    levels = jnp.arange(taps_table.shape[0], dtype=jnp.int32)
    picks = (fractions[:, None] == levels[None, :]).astype(jnp.float32)
    return jnp.dot(picks, taps_table, precision=HIGHEST)


def build_band(offsets, tap_weights, tile_width):
    source = jnp.arange(tile_width + 2 * REACH, dtype=jnp.int32)[None, :, None]
    column = jnp.arange(tile_width, dtype=jnp.int32)[None, None, :]
    lag_taps = source - column - REACH - offsets[:, None, None] + 1
    banded = jnp.zeros((offsets.shape[0], tile_width + 2 * REACH, tile_width), jnp.float32)
    for tap_index in range(tap_weights.shape[1]):
        banded = banded + jnp.where(
            lag_taps == tap_index, tap_weights[:, tap_index][:, None, None], 0.0
        )
    return banded


def combine_front(earlier, later):
    return (earlier[0] + jnp.exp(-earlier[1]) * later[0], earlier[1] + later[1])


def combine_back(earlier, later):
    return (later[0] + jnp.exp(-later[1]) * earlier[0], earlier[1] + later[1])


def with_margins(fields):
    blank = jnp.zeros(fields.shape[:3] + (1, REACH), jnp.float32)
    left_part = jnp.concatenate([blank, fields[:, :, :, :-1, -REACH:]], axis=3)
    right_part = jnp.concatenate([fields[:, :, :, 1:, :REACH], blank], axis=3)
    widened = jnp.concatenate([left_part, fields, right_part], axis=4)
    return widened


def fold_margins(spread, tile_width):
    left_rim = spread[:, :, :, :, :REACH]
    right_rim = spread[:, :, :, :, tile_width + REACH :]
    centre = spread[:, :, :, :, REACH : tile_width + REACH]
    blank = jnp.zeros(left_rim.shape[:3] + (1, REACH), jnp.float32)
    from_right = jnp.concatenate([left_rim[:, :, :, 1:], blank], axis=3)
    from_left = jnp.concatenate([blank, right_rim[:, :, :, :-1]], axis=3)
    spacing = ((0, 0), (0, 0), (0, 0), (0, 0))
    tail_part = jnp.pad(from_right, spacing + ((tile_width - REACH, 0),))
    head_part = jnp.pad(from_left, spacing + ((0, tile_width - REACH),))
    return centre + head_part + tail_part


def body(emission, absorption, target, shift_whole, shift_fraction, taps_table):
    tile_width = emission.shape[2]
    total_planes = emission.shape[0] * lax.axis_size("depth")
    fields = jnp.stack([emission, absorption])
    tile_count = lax.axis_size("lat")
    fields, goals = (
        lax.all_to_all(fields, "lat", split_axis=2, concat_axis=3, tiled=True),
        lax.all_to_all(target[None], "lat", split_axis=2, concat_axis=3, tiled=True),
    )
    fields = fields.reshape(fields.shape[:3] + (tile_count, tile_width))
    goals = goals[0].reshape(goals.shape[1:3] + (tile_count, tile_width))
    first_moment = jnp.zeros_like(fields)
    second_moment = jnp.zeros_like(fields)
    for view_index in range(ITERS):
        tap_weights = plane_taps(shift_fraction[view_index], taps_table)
        banded = build_band(shift_whole[view_index], tap_weights, tile_width)
        sheared = jnp.einsum("czrtj,zjx->czrtx", with_margins(fields), banded, precision=HIGHEST)
        color_raw = sheared[0]
        density = sheared[1]
        optical = jax.nn.softplus(density) / total_planes
        transmit_local = jnp.exp(optical - jnp.cumsum(optical, axis=0))
        opacity = -jnp.expm1(-optical)
        emitted = transmit_local * opacity * color_raw
        slab_light = jnp.sum(emitted, axis=0)
        slab_depth = jnp.sum(optical, axis=0)
        blank = jnp.zeros_like(slab_light)
        front_light, front_depth = carried_in(
            (slab_light, slab_depth), "depth", combine_front, (blank, blank), False
        )
        attenuate = jnp.exp(-front_depth)
        back_light, back_depth = carried_in(
            (slab_light, slab_depth), "depth", combine_back, (blank, blank), True
        )
        rendered = front_light + attenuate * (slab_light + jnp.exp(-slab_depth) * back_light)
        residual = rendered - goals[view_index]
        transmit = attenuate * transmit_local
        behind = rendered - front_light - attenuate * jnp.cumsum(emitted, axis=0)
        grad_color = total_planes * residual * transmit * opacity
        grad_density = (
            residual * (transmit * jnp.exp(-optical) * color_raw - behind) * jax.nn.sigmoid(density)
        )
        spread = jnp.einsum(
            "czrtx,zjx->czrtj", jnp.stack([grad_color, grad_density]), banded, precision=HIGHEST
        )
        gradient = fold_margins(spread, tile_width)
        step_number = view_index + 1
        first_moment = BETA_FIRST * first_moment + (1.0 - BETA_FIRST) * gradient
        second_moment = BETA_SECOND * second_moment + (1.0 - BETA_SECOND) * gradient * gradient
        scaled_first = first_moment / (1.0 - BETA_FIRST**step_number)
        scaled_second = second_moment / (1.0 - BETA_SECOND**step_number)
        fields = fields - LEARN_RATE * scaled_first / (jnp.sqrt(scaled_second) + ADAM_EPSILON)
    fields = fields.reshape(fields.shape[:3] + (fields.shape[3] * tile_width,))
    fields = lax.all_to_all(fields, "lat", split_axis=3, concat_axis=2, tiled=True)
    return (fields[0], fields[1])


def solution(mesh):
    in_specs = (
        P("depth", None, "lat"),
        P("depth", None, "lat"),
        P(None, None, "lat"),
        P(None, "depth"),
        P(None, "depth"),
        P(),
    )
    out_specs = (P("depth", None, "lat"), P("depth", None, "lat"))
    return jax.shard_map(body, mesh=mesh, in_specs=in_specs, out_specs=out_specs, check_vma=False)
```

profile of v0, /device:TPU:0, one launch (start us, length us, event | category | flops | bytes accessed | tf_op | source)
XLA Modules:
  0.0 288.7 jit_solution(7464354828743110071)
XLA Ops:
  0.6 1.6 copy.199
  2.2 1.6 copy.200
  3.8 3.2 %pad_maximum_fusion = f32[2,128,16,128]{3,0,1,2:T(2,128)} fusion(f32[1,128,16,128]{3,0,1,2:T(1,128)S(1)} %bitcast.608, f32[1,128,16,128]{3,0,1,2:T(1,128)S(1)} %bitcast.607), kind=kLoop, calls=%fused_computation.74 | loop fusion | flops 524288 | bytes 4194304 | tf_op jit(solution)/shard_map/stack | solution.py:125
  7.0 8.1 %all-to-all-start = ((f32[2,128,16,128]{3,0,1,2:T(2,128)}), f32[2,128,16,128]{3,0,1,2:T(2,128)S(1)}, u32[]{:S(2)}, u32[]{:S(2)}) async-start(f32[2,128,16,128]{3,0,1,2:T(2,128)} %pad_maximum_fusion), calls=%async_computation | async-start | bytes 4194304 | tf_op jit(solution)/shard_map/all_to_all | solution.py:128
  16.6 30.3 %all-to-all-done = f32[2,128,16,128]{3,0,1,2:T(2,128)S(1)} async-done(((f32[2,128,16,128]{3,0,1,2:T(2,128)}), f32[2,128,16,128]{3,0,1,2:T(2,128)S(1)}, u32[]{:S(2)}, u32[]{:S(2)}) %all-to-all-start) | async-done | bytes 2097184 | tf_op jit(solution)/shard_map/all_to_all | solution.py:128
  46.9 3.7 %all-to-all-start.2 = ((f32[1,3,16,128]{3,0,1,2:T(1,128)}), f32[1,3,16,128]{3,0,1,2:T(1,128)S(1)}, u32[]{:S(2)}, u32[]{:S(2)}) async-start(f32[1,3,16,128]{3,0,1,2:T(1,128)} %copy.206), calls=%async_computation.2 | async-start | bytes 49152 | tf_op jit(solution)/shard_map/all_to_all | solution.py:129
  52.6 17.9 %fusion.58 = f32[2,128,1,16,128]{4,3,0,1,2:T(8,128)S(1)} fusion(f32[2,128,1,15,32]{4,3,0,1,2:T(8,128)S(1)} %get-tuple-element.37, f32[2,128,1,15,32]{4,3,0,1,2:T(8,128)S(1)} %get-tuple-element.36, f32[2,128,1,16,128]{4,3,0,1,2:T(8,128)S(1)} %bitcast.603, f32[128]{0:T(128)S(1)} %get-tuple-element.115, f32[128]{0:T(128)S(1)} %get-tuple-element.116, ...), kind=kOutput, calls=%fused_computation.91 | convolution fusion | flops 1253572608 | bytes 5278208 | tf_op jit(solution)/shard_map/czrtj,zjx->czrtx/dot_general | solution.py:138
  72.4 4.5 %all-to-all-start.1 = ((f32[8,32,128]{2,1,0:T(8,128)}), f32[8,32,128]{2,1,0:T(8,128)S(1)}, u32[]{:S(2)}, u32[]{:S(2)}) async-start(f32[8,32,128]{2,1,0:T(8,128)} %broadcast_in_dim.227), calls=%async_computation.1 | async-start | bytes 262144 | tf_op jit(solution)/shard_map/all_to_all | solution.py:17
  76.9 6.1 %all-to-all-done.1 = f32[8,32,128]{2,1,0:T(8,128)S(1)} async-done(((f32[8,32,128]{2,1,0:T(8,128)}), f32[8,32,128]{2,1,0:T(8,128)S(1)}, u32[]{:S(2)}, u32[]{:S(2)}) %all-to-all-start.1) | async-done | bytes 131104 | tf_op jit(solution)/shard_map/all_to_all | solution.py:17
  84.4 1.5 fusion.106
  85.9 26.7 %fusion.33 = f32[2,128,1,16,192]{4,3,0,1,2:T(8,128)S(1)} fusion(f32[128]{0:T(128)S(1)} %get-tuple-element.115, f32[128]{0:T(128)S(1)} %get-tuple-element.116, f32[128]{0:T(128)S(1)} %get-tuple-element.117, f32[128]{0:T(128)S(1)} %get-tuple-element.114, s32[128]{0:T(128)S(1)} %get-tuple-element.101, s32[192,128]{1,0:T(8,128)S(1)} %subtract_add_fusion.3, ...), kind=kOutput, calls=%fused_computation.55 | convolution fusion | flops 1249378304 | bytes 5343744 | tf_op jit(solution)/shard_map/czrtx,zjx->czrtj/dot_general | solution.py:163
  114.2 3.8 %divide_subtract_fusion.1 = (f32[2,128,1,16,128]{4,3,0,1,2:T(8,128)S(1)}, f32[2,128,1,16,128]{4,3,0,1,2:T(8,128)}) fusion(f32[2,128,16,128]{3,0,1,2:T(2,128)S(1)} %copy-done.3, f32[2,128,1,15,32]{4,3,0,1,2:T(8,128)S(1)} %get-tuple-element.29, f32[2,128,1,15,32]{4,3,0,1,2:T(8,128)S(1)} %get-tuple-element.28, f32[2,128,1,16,192]{4,3,0,1,2:T(8,128)S(1)} %fusion.33), kind=kLoop, calls=%fused_computation.90 | loop fusion | flops 4718592 | bytes 9371648 | tf_op jit(solution)/shard_map/sub | solution.py:172
  118.8 17.5 %fusion.63 = f32[2,128,1,16,128]{4,3,1,2,0:T(8,128)S(1)} fusion(f32[128]{0:T(128)S(1)} %get-tuple-element.111, f32[128]{0:T(128)S(1)} %get-tuple-element.112, f32[128]{0:T(128)S(1)} %get-tuple-element.113, f32[128]{0:T(128)S(1)} %get-tuple-element.110, s32[128]{0:T(128)S(1)} %get-tuple-element.102, s32[192,128]{1,0:T(8,128)S(1)} %subtract_add_fusion.3, ...), kind=kOutput, calls=%fused_computation.92 | convolution fusion | flops 1253572608 | bytes 5278208 | tf_op jit(solution)/shard_map/czrtj,zjx->czrtx/dot_general | solution.py:138
  138.2 3.4 %all-to-all-start.3 = ((f32[8,32,128]{2,1,0:T(8,128)}), f32[8,32,128]{2,1,0:T(8,128)S(1)}, u32[]{:S(2)}, u32[]{:S(2)}) async-start(f32[8,32,128]{2,1,0:T(8,128)} %broadcast_in_dim.239), calls=%async_computation.3 | async-start | bytes 262144 | tf_op jit(solution)/shard_map/all_to_all | solution.py:17
  141.6 6.0 %all-to-all-done.3 = f32[8,32,128]{2,1,0:T(8,128)S(1)} async-done(((f32[8,32,128]{2,1,0:T(8,128)}), f32[8,32,128]{2,1,0:T(8,128)S(1)}, u32[]{:S(2)}, u32[]{:S(2)}) %all-to-all-start.3) | async-done | bytes 131104 | tf_op jit(solution)/shard_map/all_to_all | solution.py:17
  150.5 26.8 %fusion.36 = f32[2,128,1,16,192]{4,3,0,1,2:T(8,128)S(1)} fusion(f32[128]{0:T(128)S(1)} %get-tuple-element.111, f32[128]{0:T(128)S(1)} %get-tuple-element.112, f32[128]{0:T(128)S(1)} %get-tuple-element.113, f32[128]{0:T(128)S(1)} %get-tuple-element.110, s32[128]{0:T(128)S(1)} %get-tuple-element.102, s32[192,128]{1,0:T(8,128)S(1)} %subtract_add_fusion.3, ...), kind=kOutput, calls=%fused_computation.56 | convolution fusion | flops 1249378304 | bytes 5343744 | tf_op jit(solution)/shard_map/czrtx,zjx->czrtj/dot_general | solution.py:163
  179.6 4.6 %divide_subtract_fusion = f32[2,128,1,16,128]{4,3,0,1,2:T(8,128)S(1)} fusion(f32[2,128,1,16,128]{4,3,0,1,2:T(8,128)S(1)} %copy-done.5, f32[2,128,1,15,32]{4,3,0,1,2:T(8,128)S(1)} %get-tuple-element.27, f32[2,128,1,15,32]{4,3,0,1,2:T(8,128)S(1)} %get-tuple-element.26, f32[2,128,1,16,192]{4,3,0,1,2:T(8,128)S(1)} %fusion.36, f32[2,128,16,128]{3,0,1,2:T(2,128)S(1)} %copy-done.4), kind=kLoop, calls=%fused_computation.88 | loop fusion | flops 11010048 | bytes 9371648 | tf_op jit(solution)/shard_map/sub | solution.py:172
  185.0 17.5 %fusion.68 = f32[2,128,1,16,128]{4,3,1,2,0:T(8,128)S(1)} fusion(f32[128]{0:T(128)S(1)} %get-tuple-element.104, f32[128]{0:T(128)S(1)} %get-tuple-element.105, f32[128]{0:T(128)S(1)} %get-tuple-element.106, f32[128]{0:T(128)S(1)} %get-tuple-element.103, s32[128]{0:T(128)S(1)} %get-tuple-element.100, s32[192,128]{1,0:T(8,128)S(1)} %subtract_add_fusion.3, ...), kind=kOutput, calls=%fused_computation.93 | convolution fusion | flops 1253572608 | bytes 5278208 | tf_op jit(solution)/shard_map/czrtj,zjx->czrtx/dot_general | solution.py:138
  203.7 8.7 %all_to_all.48 = f32[8,32,128]{2,1,0:T(8,128)S(1)} all-to-all(f32[8,32,128]{2,1,0:T(8,128)S(1)} %broadcast_in_dim.248), channel_id=1, replica_groups=mesh['depth'=8,'lat'=16] {'depth'}, dimensions={0} | all-to-all | bytes 262144 | tf_op jit(solution)/shard_map/all_to_all | solution.py:17
  215.3 26.5 %fusion.39 = f32[2,128,1,16,192]{4,3,0,1,2:T(8,128)S(1)} fusion(f32[128]{0:T(128)S(1)} %get-tuple-element.104, f32[128]{0:T(128)S(1)} %get-tuple-element.105, f32[128]{0:T(128)S(1)} %get-tuple-element.106, f32[128]{0:T(128)S(1)} %get-tuple-element.103, s32[128]{0:T(128)S(1)} %get-tuple-element.100, s32[192,128]{1,0:T(8,128)S(1)} %subtract_add_fusion.3, ...), kind=kOutput, calls=%fused_computation.57 | convolution fusion | flops 1249378304 | bytes 5343744 | tf_op jit(solution)/shard_map/czrtx,zjx->czrtj/dot_general | solution.py:163
  242.6 4.0 %fusion.48 = f32[2,128,1,16,128]{4,3,0,1,2:T(8,128)S(1)} fusion(f32[2,128,1,16,128]{4,3,0,1,2:T(8,128)S(1)} %divide_subtract_fusion, f32[2,128,1,15,32]{4,3,0,1,2:T(8,128)S(1)} %get-tuple-element.25, f32[2,128,1,15,32]{4,3,0,1,2:T(8,128)S(1)} %get-tuple-element.24, f32[2,128,1,16,192]{4,3,0,1,2:T(8,128)S(1)} %fusion.39, ...), kind=kLoop, calls=%fused_computation.64 | loop fusion | flops 13107200 | bytes 12451840 | tf_op jit(solution)/shard_map/sub | solution.py:172
  246.6 1.9 copy.258
  248.5 35.5 %all_to_all.49 = f32[2,128,1,2048]{1,0,2,3:T(2,128)S(1)} all-to-all(f32[2,128,1,2048]{1,0,2,3:T(2,128)} %bitcast.604), channel_id=1, replica_groups=mesh['depth'=8,'lat'=16] {'lat'}, dimensions={3} | all-to-all | bytes 4194304 | tf_op jit(solution)/shard_map/all_to_all | solution.py:174
  284.0 1.6 fusion.265
  (86 shorter events, 24.3 us)
Async XLA Ops:
  0.6 15.2 %copy-start = (f32[8,4]{0,1:T(4,128)S(1)}, f32[8,4]{0,1:T(4,128)}, u32[]{:S(2)}) copy-start(f32[8,4]{0,1:T(4,128)} %param.11) | copy-start | bytes 388
  7.0 8.1 %copy-start.6 = (f32[3,16,128]{2,1,0:T(8,128)S(1)}, f32[3,16,128]{2,1,0:T(8,128)}, u32[]{:S(2)}) copy-start(f32[3,16,128]{2,1,0:T(8,128)} %param.8) | copy-start | bytes 73732
  7.0 8.8 %copy-start.7 = (s32[3,128]{1,0:T(4,128)S(1)}, s32[3,128]{1,0:T(4,128)}, u32[]{:S(2)}) copy-start(s32[3,128]{1,0:T(4,128)} %param.9) | copy-start | bytes 4612
  7.0 8.8 %copy-start.8 = (s32[3,128]{1,0:T(4,128)S(1)}, s32[3,128]{1,0:T(4,128)}, u32[]{:S(2)}) copy-start(s32[3,128]{1,0:T(4,128)} %param.10) | copy-start | bytes 4612
  7.0 39.9 %all-to-all-start = ((f32[2,128,16,128]{3,0,1,2:T(2,128)}), f32[2,128,16,128]{3,0,1,2:T(2,128)S(1)}, u32[]{:S(2)}, u32[]{:S(2)}) async-start(f32[2,128,16,128]{3,0,1,2:T(2,128)} %pad_maximum_fusion), calls=%async_computation | async-start | bytes 4194304 | tf_op jit(solution)/shard_map/all_to_all | solution.py:128
  46.9 5.7 %copy-start.2 = (f32[2,128,16,128]{3,0,1,2:T(2,128)}, f32[2,128,16,128]{3,0,1,2:T(2,128)S(1)}, u32[]{:S(2)}) copy-start(f32[2,128,16,128]{3,0,1,2:T(2,128)S(1)} %all-to-all-done) | copy-start | bytes 6291460
  46.9 24.8 %all-to-all-start.2 = ((f32[1,3,16,128]{3,0,1,2:T(1,128)}), f32[1,3,16,128]{3,0,1,2:T(1,128)S(1)}, u32[]{:S(2)}, u32[]{:S(2)}) async-start(f32[1,3,16,128]{3,0,1,2:T(1,128)} %copy.206), calls=%async_computation.2 | async-start | bytes 49152 | tf_op jit(solution)/shard_map/all_to_all | solution.py:129
  72.4 10.6 %all-to-all-start.1 = ((f32[8,32,128]{2,1,0:T(8,128)}), f32[8,32,128]{2,1,0:T(8,128)S(1)}, u32[]{:S(2)}, u32[]{:S(2)}) async-start(f32[8,32,128]{2,1,0:T(8,128)} %broadcast_in_dim.227), calls=%async_computation.1 | async-start | bytes 262144 | tf_op jit(solution)/shard_map/all_to_all | solution.py:17
  112.6 1.6 copy-start.3
  138.2 9.4 %all-to-all-start.3 = ((f32[8,32,128]{2,1,0:T(8,128)}), f32[8,32,128]{2,1,0:T(8,128)S(1)}, u32[]{:S(2)}, u32[]{:S(2)}) async-start(f32[8,32,128]{2,1,0:T(8,128)} %broadcast_in_dim.239), calls=%async_computation.3 | async-start | bytes 262144 | tf_op jit(solution)/shard_map/all_to_all | solution.py:17
  177.3 1.6 copy-start.4
  177.4 2.2 copy-start.5
  284.0 4.4 %copy-start.1 = (f32[8,4]{0,1:T(4,128)S(1)}, f32[8,4]{0,1:T(4,128)}, u32[]{:S(2)}) copy-start(f32[8,4]{0,1:T(4,128)} %param.11) | copy-start | bytes 388
where the time goes:
time: 292 us; the launch traced here: 289 us
  matrix products  134 us (46%)
  blocking collectives  44.2 us (15%)
  waiting for transfers between devices  42.4 us (15%)
  other arithmetic  27.7 us (9%)
  local copies, waits for them, and re-layouts  19.7 us (7%)
  starting transfers between devices  19.6 us (7%)
    dot_general x3, matrix products, body(): jnp.einsum('czrtx,zjx->czrtj', jnp.stack([grad_color, grad_density]), ban...  80 us
    dot_general x3, matrix products, body(): jnp.einsum('czrtj,zjx->czrtx', with_margins(fields), banded, precision=HI...  52.9 us
    all_to_all x1, blocking collectives, body(): lax.all_to_all(fields, 'lat', split_axis=3, concat_axis=2, tiled=True)  35.5 us
    all_to_all x1, waiting for transfers between devices, body(): lax.all_to_all(fields, 'lat', split_axis=2, concat_axis=3, tiled=True)  30.3 us
    sub x3, other arithmetic, body(): fields - LEARN_RATE * scaled_first / (jnp.sqrt(scaled_second) + ADAM_EPSI...  12.4 us
    all_to_all x2, waiting for transfers between devices, copy_for_each(): lax.all_to_all(jnp.broadcast_to(x[None], (devices, *x.shape)), axis, 0, 0...  12.1 us
    all_to_all x1, blocking collectives, copy_for_each(): lax.all_to_all(jnp.broadcast_to(x[None], (devices, *x.shape)), axis, 0, 0...  8.7 us
    all_to_all x1, starting transfers between devices, body(): lax.all_to_all(fields, 'lat', split_axis=2, concat_axis=3, tiled=True)  8.12 us
  transfers between devices with their start and end apart: 4, of which 3 were waited for; matrix products, arithmetic and copies ran while one was open for 8% of the time, Pallas kernels for 0%

commit v1 on v0

--- a/solution.py
+++ b/solution.py
@@ -171,7 +171,10 @@
         scaled_second = second_moment / (1.0 - BETA_SECOND**step_number)
         fields = fields - LEARN_RATE * scaled_first / (jnp.sqrt(scaled_second) + ADAM_EPSILON)
     fields = fields.reshape(fields.shape[:3] + (fields.shape[3] * tile_width,))
-    fields = lax.all_to_all(fields, "lat", split_axis=3, concat_axis=2, tiled=True)
+    size = lax.axis_size("lat")
+    blocks = jnp.stack(jnp.split(fields, size, axis=3), axis=0)
+    blocks = lax.all_to_all(blocks, "lat", split_axis=0, concat_axis=0)
+    fields = jnp.concatenate(blocks, axis=2)
     return (fields[0], fields[1])
 
 

time: 292 us -> 292 us (level)
    unnamed x22 -> x39, local copies, waits for them, and re-layouts: 8.02 us -> 7.47 us
where the time goes in v1:
time: 292 us; the launch traced here: 289 us
  matrix products  134 us (46%)
  blocking collectives  44 us (15%)
  waiting for transfers between devices  42.4 us (15%)
  other arithmetic  27.7 us (9%)
  local copies, waits for them, and re-layouts  19.8 us (7%)
  starting transfers between devices  19.6 us (7%)
    dot_general x3, matrix products, body(): jnp.einsum('czrtx,zjx->czrtj', jnp.stack([grad_color, grad_density]), ban...  80 us
    dot_general x3, matrix products, body(): jnp.einsum('czrtj,zjx->czrtx', with_margins(fields), banded, precision=HI...  52.9 us
    all_to_all x1, blocking collectives, body(): blocks = lax.all_to_all(blocks, 'lat', split_axis=0, concat_axis=0)  35.3 us
    all_to_all x1, waiting for transfers between devices, body(): lax.all_to_all(fields, 'lat', split_axis=2, concat_axis=3, tiled=True)  30.3 us
    sub x3, other arithmetic, body(): fields - LEARN_RATE * scaled_first / (jnp.sqrt(scaled_second) + ADAM_EPSI...  12.4 us
    all_to_all x2, waiting for transfers between devices, copy_for_each(): lax.all_to_all(jnp.broadcast_to(x[None], (devices, *x.shape)), axis, 0, 0...  12.1 us
    all_to_all x1, blocking collectives, copy_for_each(): lax.all_to_all(jnp.broadcast_to(x[None], (devices, *x.shape)), axis, 0, 0...  8.7 us
    all_to_all x1, starting transfers between devices, body(): lax.all_to_all(fields, 'lat', split_axis=2, concat_axis=3, tiled=True)  8.12 us
  transfers between devices with their start and end apart: 4, of which 3 were waited for; matrix products, arithmetic and copies ran while one was open for 8% of the time, Pallas kernels for 0%

profile of v1, /device:TPU:0, one launch (start us, length us, event | category | flops | bytes accessed | tf_op | source)
XLA Modules:
  0.0 288.8 jit_solution(6395481755524939896)
XLA Ops:
  0.7 1.7 copy.256
  2.7 3.2 %pad_maximum_fusion = f32[2,128,16,128]{3,0,1,2:T(2,128)} fusion(f32[1,128,16,128]{3,0,1,2:T(1,128)S(1)} %bitcast.672, f32[1,128,16,128]{3,0,1,2:T(1,128)S(1)} %bitcast.671), kind=kLoop, calls=%fused_computation.74 | loop fusion | flops 524288 | bytes 4194304 | tf_op jit(solution)/shard_map/stack | solution.py:125
  5.9 8.1 %all-to-all-start = ((f32[2,128,16,128]{3,0,1,2:T(2,128)}), f32[2,128,16,128]{3,0,1,2:T(2,128)S(1)}, u32[]{:S(2)}, u32[]{:S(2)}) async-start(f32[2,128,16,128]{3,0,1,2:T(2,128)} %pad_maximum_fusion), calls=%async_computation | async-start | bytes 4194304 | tf_op jit(solution)/shard_map/all_to_all | solution.py:128
  15.5 30.3 %all-to-all-done = f32[2,128,16,128]{3,0,1,2:T(2,128)S(1)} async-done(((f32[2,128,16,128]{3,0,1,2:T(2,128)}), f32[2,128,16,128]{3,0,1,2:T(2,128)S(1)}, u32[]{:S(2)}, u32[]{:S(2)}) %all-to-all-start) | async-done | bytes 2097184 | tf_op jit(solution)/shard_map/all_to_all | solution.py:128
  45.8 3.7 %all-to-all-start.2 = ((f32[1,3,16,128]{3,0,1,2:T(1,128)}), f32[1,3,16,128]{3,0,1,2:T(1,128)S(1)}, u32[]{:S(2)}, u32[]{:S(2)}) async-start(f32[1,3,16,128]{3,0,1,2:T(1,128)} %copy.263), calls=%async_computation.2 | async-start | bytes 49152 | tf_op jit(solution)/shard_map/all_to_all | solution.py:129
  51.5 17.9 %fusion.58 = f32[2,128,1,16,128]{4,3,0,1,2:T(8,128)S(1)} fusion(f32[2,128,1,15,32]{4,3,0,1,2:T(8,128)S(1)} %get-tuple-element.53, f32[2,128,1,15,32]{4,3,0,1,2:T(8,128)S(1)} %get-tuple-element.52, f32[2,128,1,16,128]{4,3,0,1,2:T(8,128)S(1)} %bitcast.669, f32[128]{0:T(128)S(1)} %get-tuple-element.131, f32[128]{0:T(128)S(1)} %get-tuple-element.132, ...), kind=kOutput, calls=%fused_computation.91 | convolution fusion | flops 1253572608 | bytes 5278208 | tf_op jit(solution)/shard_map/czrtj,zjx->czrtx/dot_general | solution.py:138
  71.3 4.5 %all-to-all-start.1 = ((f32[8,32,128]{2,1,0:T(8,128)}), f32[8,32,128]{2,1,0:T(8,128)S(1)}, u32[]{:S(2)}, u32[]{:S(2)}) async-start(f32[8,32,128]{2,1,0:T(8,128)} %broadcast_in_dim.227), calls=%async_computation.1 | async-start | bytes 262144 | tf_op jit(solution)/shard_map/all_to_all | solution.py:17
  75.8 6.1 %all-to-all-done.1 = f32[8,32,128]{2,1,0:T(8,128)S(1)} async-done(((f32[8,32,128]{2,1,0:T(8,128)}), f32[8,32,128]{2,1,0:T(8,128)S(1)}, u32[]{:S(2)}, u32[]{:S(2)}) %all-to-all-start.1) | async-done | bytes 131104 | tf_op jit(solution)/shard_map/all_to_all | solution.py:17
  84.8 26.7 %fusion.33 = f32[2,128,1,16,192]{4,3,0,1,2:T(8,128)S(1)} fusion(f32[128]{0:T(128)S(1)} %get-tuple-element.131, f32[128]{0:T(128)S(1)} %get-tuple-element.132, f32[128]{0:T(128)S(1)} %get-tuple-element.133, f32[128]{0:T(128)S(1)} %get-tuple-element.130, s32[128]{0:T(128)S(1)} %get-tuple-element.117, s32[192,128]{1,0:T(8,128)S(1)} %subtract_add_fusion.3, ...), kind=kOutput, calls=%fused_computation.55 | convolution fusion | flops 1249378304 | bytes 5343744 | tf_op jit(solution)/shard_map/czrtx,zjx->czrtj/dot_general | solution.py:163
  113.1 3.8 %divide_subtract_fusion.1 = (f32[2,128,1,16,128]{4,3,0,1,2:T(8,128)S(1)}, f32[2,128,1,16,128]{4,3,0,1,2:T(8,128)}) fusion(f32[2,128,16,128]{3,0,1,2:T(2,128)S(1)} %copy-done.3, f32[2,128,1,15,32]{4,3,0,1,2:T(8,128)S(1)} %get-tuple-element.29, f32[2,128,1,15,32]{4,3,0,1,2:T(8,128)S(1)} %get-tuple-element.28, f32[2,128,1,16,192]{4,3,0,1,2:T(8,128)S(1)} %fusion.33), kind=kLoop, calls=%fused_computation.90 | loop fusion | flops 4718592 | bytes 9371648 | tf_op jit(solution)/shard_map/sub | solution.py:172
  117.7 17.5 %fusion.63 = f32[2,128,1,16,128]{4,3,1,2,0:T(8,128)S(1)} fusion(f32[128]{0:T(128)S(1)} %get-tuple-element.127, f32[128]{0:T(128)S(1)} %get-tuple-element.128, f32[128]{0:T(128)S(1)} %get-tuple-element.129, f32[128]{0:T(128)S(1)} %get-tuple-element.126, s32[128]{0:T(128)S(1)} %get-tuple-element.118, s32[192,128]{1,0:T(8,128)S(1)} %subtract_add_fusion.3, ...), kind=kOutput, calls=%fused_computation.92 | convolution fusion | flops 1253572608 | bytes 5278208 | tf_op jit(solution)/shard_map/czrtj,zjx->czrtx/dot_general | solution.py:138
  137.1 3.4 %all-to-all-start.3 = ((f32[8,32,128]{2,1,0:T(8,128)}), f32[8,32,128]{2,1,0:T(8,128)S(1)}, u32[]{:S(2)}, u32[]{:S(2)}) async-start(f32[8,32,128]{2,1,0:T(8,128)} %broadcast_in_dim.239), calls=%async_computation.3 | async-start | bytes 262144 | tf_op jit(solution)/shard_map/all_to_all | solution.py:17
  140.5 6.0 %all-to-all-done.3 = f32[8,32,128]{2,1,0:T(8,128)S(1)} async-done(((f32[8,32,128]{2,1,0:T(8,128)}), f32[8,32,128]{2,1,0:T(8,128)S(1)}, u32[]{:S(2)}, u32[]{:S(2)}) %all-to-all-start.3) | async-done | bytes 131104 | tf_op jit(solution)/shard_map/all_to_all | solution.py:17
  149.4 26.8 %fusion.36 = f32[2,128,1,16,192]{4,3,0,1,2:T(8,128)S(1)} fusion(f32[128]{0:T(128)S(1)} %get-tuple-element.127, f32[128]{0:T(128)S(1)} %get-tuple-element.128, f32[128]{0:T(128)S(1)} %get-tuple-element.129, f32[128]{0:T(128)S(1)} %get-tuple-element.126, s32[128]{0:T(128)S(1)} %get-tuple-element.118, s32[192,128]{1,0:T(8,128)S(1)} %subtract_add_fusion.3, ...), kind=kOutput, calls=%fused_computation.56 | convolution fusion | flops 1249378304 | bytes 5343744 | tf_op jit(solution)/shard_map/czrtx,zjx->czrtj/dot_general | solution.py:163
  178.5 4.6 %divide_subtract_fusion = f32[2,128,1,16,128]{4,3,0,1,2:T(8,128)S(1)} fusion(f32[2,128,1,16,128]{4,3,0,1,2:T(8,128)S(1)} %copy-done.5, f32[2,128,1,15,32]{4,3,0,1,2:T(8,128)S(1)} %get-tuple-element.27, f32[2,128,1,15,32]{4,3,0,1,2:T(8,128)S(1)} %get-tuple-element.26, f32[2,128,1,16,192]{4,3,0,1,2:T(8,128)S(1)} %fusion.36, f32[2,128,16,128]{3,0,1,2:T(2,128)S(1)} %copy-done.4), kind=kLoop, calls=%fused_computation.88 | loop fusion | flops 11010048 | bytes 9371648 | tf_op jit(solution)/shard_map/sub | solution.py:172
  183.9 17.5 %fusion.68 = f32[2,128,1,16,128]{4,3,1,2,0:T(8,128)S(1)} fusion(f32[128]{0:T(128)S(1)} %get-tuple-element.120, f32[128]{0:T(128)S(1)} %get-tuple-element.121, f32[128]{0:T(128)S(1)} %get-tuple-element.122, f32[128]{0:T(128)S(1)} %get-tuple-element.119, s32[128]{0:T(128)S(1)} %get-tuple-element.116, s32[192,128]{1,0:T(8,128)S(1)} %subtract_add_fusion.3, ...), kind=kOutput, calls=%fused_computation.93 | convolution fusion | flops 1253572608 | bytes 5278208 | tf_op jit(solution)/shard_map/czrtj,zjx->czrtx/dot_general | solution.py:138
  202.6 8.7 %all_to_all.44 = f32[8,32,128]{2,1,0:T(8,128)S(1)} all-to-all(f32[8,32,128]{2,1,0:T(8,128)S(1)} %broadcast_in_dim.248), channel_id=1, replica_groups=mesh['depth'=8,'lat'=16] {'depth'}, dimensions={0} | all-to-all | bytes 262144 | tf_op jit(solution)/shard_map/all_to_all | solution.py:17
  214.2 26.5 %fusion.39 = f32[2,128,1,16,192]{4,3,0,1,2:T(8,128)S(1)} fusion(f32[128]{0:T(128)S(1)} %get-tuple-element.120, f32[128]{0:T(128)S(1)} %get-tuple-element.121, f32[128]{0:T(128)S(1)} %get-tuple-element.122, f32[128]{0:T(128)S(1)} %get-tuple-element.119, s32[128]{0:T(128)S(1)} %get-tuple-element.116, s32[192,128]{1,0:T(8,128)S(1)} %subtract_add_fusion.3, ...), kind=kOutput, calls=%fused_computation.57 | convolution fusion | flops 1249378304 | bytes 5343744 | tf_op jit(solution)/shard_map/czrtx,zjx->czrtj/dot_general | solution.py:163
  241.5 4.0 %fusion.48 = f32[2,128,1,16,128]{4,3,0,1,2:T(8,128)S(1)} fusion(f32[2,128,1,16,128]{4,3,0,1,2:T(8,128)S(1)} %divide_subtract_fusion, f32[2,128,1,15,32]{4,3,0,1,2:T(8,128)S(1)} %get-tuple-element.25, f32[2,128,1,15,32]{4,3,0,1,2:T(8,128)S(1)} %get-tuple-element.24, f32[2,128,1,16,192]{4,3,0,1,2:T(8,128)S(1)} %fusion.39, ...), kind=kLoop, calls=%fused_computation.64 | loop fusion | flops 13107200 | bytes 12451840 | tf_op jit(solution)/shard_map/sub | solution.py:172
  245.5 2.1 reshape.865
  247.6 1.9 fusion.281
  249.8 35.3 %all_to_all.45 = f32[16,2,128,1,128]{4,2,3,1,0:T(8,128)S(1)} all-to-all(f32[16,2,128,1,128]{4,2,3,1,0:T(8,128)S(1)} %fusion.166), channel_id=1, replica_groups=mesh['depth'=8,'lat'=16] {'lat'}, dimensions={0} | all-to-all | bytes 4194304 | tf_op jit(solution)/shard_map/all_to_all | solution.py:176
  285.3 1.6 copy.320
  286.9 1.6 copy.319
  (105 shorter events, 23.8 us)
Async XLA Ops:
  0.6 14.1 %copy-start = (f32[8,4]{0,1:T(4,128)S(1)}, f32[8,4]{0,1:T(4,128)}, u32[]{:S(2)}) copy-start(f32[8,4]{0,1:T(4,128)} %param.11) | copy-start | bytes 388
  0.6 1.7 copy-start.6
  5.9 8.1 %copy-start.7 = (f32[3,16,128]{2,1,0:T(8,128)S(1)}, f32[3,16,128]{2,1,0:T(8,128)}, u32[]{:S(2)}) copy-start(f32[3,16,128]{2,1,0:T(8,128)} %param.8) | copy-start | bytes 73732
  5.9 8.8 %copy-start.8 = (s32[3,128]{1,0:T(4,128)S(1)}, s32[3,128]{1,0:T(4,128)}, u32[]{:S(2)}) copy-start(s32[3,128]{1,0:T(4,128)} %param.9) | copy-start | bytes 4612
  5.9 8.8 %copy-start.9 = (s32[3,128]{1,0:T(4,128)S(1)}, s32[3,128]{1,0:T(4,128)}, u32[]{:S(2)}) copy-start(s32[3,128]{1,0:T(4,128)} %param.10) | copy-start | bytes 4612
  5.9 39.9 %all-to-all-start = ((f32[2,128,16,128]{3,0,1,2:T(2,128)}), f32[2,128,16,128]{3,0,1,2:T(2,128)S(1)}, u32[]{:S(2)}, u32[]{:S(2)}) async-start(f32[2,128,16,128]{3,0,1,2:T(2,128)} %pad_maximum_fusion), calls=%async_computation | async-start | bytes 4194304 | tf_op jit(solution)/shard_map/all_to_all | solution.py:128
  45.8 4.9 %copy-start.2 = (f32[2,128,16,128]{3,0,1,2:T(2,128)}, f32[2,128,16,128]{3,0,1,2:T(2,128)S(1)}, u32[]{:S(2)}) copy-start(f32[2,128,16,128]{3,0,1,2:T(2,128)S(1)} %all-to-all-done) | copy-start | bytes 6291460
  45.8 24.8 %all-to-all-start.2 = ((f32[1,3,16,128]{3,0,1,2:T(1,128)}), f32[1,3,16,128]{3,0,1,2:T(1,128)S(1)}, u32[]{:S(2)}, u32[]{:S(2)}) async-start(f32[1,3,16,128]{3,0,1,2:T(1,128)} %copy.263), calls=%async_computation.2 | async-start | bytes 49152 | tf_op jit(solution)/shard_map/all_to_all | solution.py:129
  71.3 10.6 %all-to-all-start.1 = ((f32[8,32,128]{2,1,0:T(8,128)}), f32[8,32,128]{2,1,0:T(8,128)S(1)}, u32[]{:S(2)}, u32[]{:S(2)}) async-start(f32[8,32,128]{2,1,0:T(8,128)} %broadcast_in_dim.227), calls=%async_computation.1 | async-start | bytes 262144 | tf_op jit(solution)/shard_map/all_to_all | solution.py:17
  111.5 1.6 copy-start.3
  137.1 9.4 %all-to-all-start.3 = ((f32[8,32,128]{2,1,0:T(8,128)}), f32[8,32,128]{2,1,0:T(8,128)S(1)}, u32[]{:S(2)}, u32[]{:S(2)}) async-start(f32[8,32,128]{2,1,0:T(8,128)} %broadcast_in_dim.239), calls=%async_computation.3 | async-start | bytes 262144 | tf_op jit(solution)/shard_map/all_to_all | solution.py:17
  176.2 1.6 copy-start.4
  176.3 2.2 copy-start.5
  285.3 3.2 %copy-start.1 = (f32[8,4]{0,1:T(4,128)S(1)}, f32[8,4]{0,1:T(4,128)}, u32[]{:S(2)}) copy-start(f32[8,4]{0,1:T(4,128)} %param.11) | copy-start | bytes 388
